TPU v7x, 32 devices: a whole 2x2x4 slice. The times are simulated.
32 devices in a mesh: tp: 8 (over z, core), seq: 4 (over y, x).
Axes of the slice: x: 2, y: 2, z: 4, core: 2. Of those that a mesh axis runs over, the one named last changes fastest.
Arguments:
- residual: bfloat16 [1024, 4096], P('seq'), may hold values from -6 to 6
- mix_gain: float32 [4096], replicated, may hold values from 0.5 to 1.5
- in_proj: bfloat16 [4096, 4096], P(None, 'tp'), may hold values from -0.09375 to 0.09375
- branch_proj: bfloat16 [4096, 4096], P(None, 'tp'), may hold values from -0.09375 to 0.09375
- conv_weight: float32 [4, 4096], P(None, 'tp'), may hold values from -3 to 3
- conv_bias: float32 [4096], P('tp'), may hold values from -1.25 to 1.25
- input_gate: bfloat16 [16, 256, 256], P('tp'), may hold values from -0.375 to 0.375
- input_bias: float32 [4096], P('tp'), may hold values from -3 to 3
- decay_gate: bfloat16 [16, 256, 256], P('tp'), may hold values from -0.375 to 0.375
- decay_bias: float32 [4096], P('tp'), may hold values from -3 to 3
- decay_param: float32 [4096], P('tp'), may hold values from -13 to -2, as said below
- out_proj: bfloat16 [4096, 4096], P('tp'), may hold values from -0.25 to 0.25
- mlp_gain: float32 [4096], replicated, may hold values from 0.5 to 1.5
- gate_proj: bfloat16 [4096, 12288], P('seq', 'tp'), may hold values from -0.09375 to 0.09375
- up_proj: bfloat16 [4096, 12288], P('seq', 'tp'), may hold values from -0.09375 to 0.09375
- down_proj: bfloat16 [12288, 4096], P('tp'), may hold values from -0.078125 to 0.078125
Outputs:
- updated: bfloat16 [1024, 4096], P('seq')
Inputs may be any that keep to these rules, and one draw needn't show every extreme that they name: softplus(decay_param) lies between 0.02 / 1024 and 0.1 for every channel.
All inputs are finite; a program needn't handle non-finite values.
Results may differ from a plain program's by a relative error of at most 0.02.
Values may be sent and summed in bfloat16 or wider, within the bound.
A program may use at most 128 MiB of HBM per device.

v0:
```python
import jax
import jax.numpy as jnp
from jax import lax
from jax.sharding import PartitionSpec as P

epsilon = 1e-06


def from_behind(value, axis, steps):
    count = lax.axis_size(axis)
    leading, last = max(0, -steps), min(count, count - steps)
    return lax.ppermute(value, axis, [(source, source + steps) for source in range(leading, last)])


def carried_in(shard, axis, combine, identity, reverse):
    count, mine = lax.axis_size(axis), lax.axis_index(axis)
    everything = jax.tree.map(lambda part: lax.all_gather(part, axis), shard)
    start = jax.tree.map(
        lambda part, zero: jnp.broadcast_to(jnp.asarray(zero, part.dtype), part.shape),
        shard,
        identity,
    )

    def lap(k, before):
        at = count - 1 - k if reverse else k
        reached = at > mine if reverse else at < mine
        new = combine(before, jax.tree.map(lambda part: part[at], everything))
        return jax.tree.map(lambda a, b: jnp.where(reached, a, b), new, before)

    return lax.fori_loop(0, count, lap, start)


def summed_rows(product, extent, axis):
    everything = product(jnp.int32(0), lax.axis_size(axis) * extent)
    own = lax.psum_scatter(everything.astype(jnp.bfloat16), axis, scatter_dimension=0, tiled=True)
    return own.astype(jnp.float32)


def rms_norm(values, gain):
    wide = values.astype(jnp.float32)
    factor = lax.rsqrt(jnp.mean(wide * wide, axis=-1, keepdims=True) + epsilon)
    return (wide * factor * gain).astype(jnp.bfloat16)


def block_gates(values, weight, bias):
    heads, width = (weight.shape[0], weight.shape[1])
    grouped = values.reshape(values.shape[0], heads, width)
    mixed = jnp.einsum("thi,hij->thj", grouped, weight, preferred_element_type=jnp.float32)
    return jax.nn.sigmoid(mixed.reshape(values.shape[0], heads * width) + bias)


def smooth(inner, tail, conv_weight, conv_bias):
    taps = conv_weight.shape[0]
    length = inner.shape[0]
    padded = jnp.concatenate([tail, inner], axis=0).astype(jnp.float32)
    total = conv_bias + jnp.zeros((length, inner.shape[1]), jnp.float32)
    for offset in range(taps):
        total = total + conv_weight[offset] * padded[taps - 1 - offset : taps - 1 - offset + length]
    return lax.optimization_barrier(total.astype(jnp.bfloat16))


def combine_state(earlier, later):
    return (earlier[0] * later[0], later[0] * earlier[1] + later[1])


def channel_total(partial_value):
    return lax.psum(partial_value.astype(jnp.bfloat16), "tp").astype(jnp.float32)


def on_device(
    residual,
    mix_gain,
    in_proj,
    branch_proj,
    conv_weight,
    conv_bias,
    input_gate,
    input_bias,
    decay_gate,
    decay_bias,
    decay_param,
    out_proj,
    mlp_gain,
    gate_proj,
    up_proj,
    down_proj,
):
    length = residual.shape[0]
    taps = conv_weight.shape[0]
    normed = rms_norm(residual, mix_gain)
    branch = jax.nn.gelu(
        jnp.dot(normed, branch_proj, preferred_element_type=jnp.float32), approximate=True
    )
    inner = jnp.dot(normed, in_proj, preferred_element_type=jnp.float32).astype(jnp.bfloat16)
    tail = from_behind(inner[length - (taps - 1) :], "seq", 1)
    smoothed = smooth(inner, tail, conv_weight, conv_bias)
    input_rate = block_gates(smoothed, input_gate, input_bias)
    decay_rate = block_gates(smoothed, decay_gate, decay_bias)
    log_decay = -8.0 * decay_rate * jax.nn.softplus(decay_param)
    decay = jnp.exp(log_decay)
    position = lax.axis_index("seq")
    first = jnp.logical_and(position == 0, jnp.arange(length) == 0)[:, None]
    scale_in = jnp.where(first, 1.0, jnp.sqrt(-jnp.expm1(2.0 * log_decay)))
    pushed = smoothed.astype(jnp.float32) * input_rate * scale_in
    decays, partial_states = lax.associative_scan(combine_state, (decay, pushed), axis=0)
    end_decay = decays[-1]
    end_state = partial_states[-1]
    carried = carried_in(
        (end_decay, end_state),
        "seq",
        combine_state,
        (jnp.ones_like(end_decay), jnp.zeros_like(end_state)),
        False,
    )[1]
    states = partial_states + decays * carried[None]
    gated = (states * branch).astype(jnp.bfloat16)
    mixed = channel_total(jnp.dot(gated, out_proj, preferred_element_type=jnp.float32))
    middle = lax.optimization_barrier((residual.astype(jnp.float32) + mixed).astype(jnp.bfloat16))
    hidden_in = rms_norm(middle, mlp_gain)
    width = gate_proj.shape[1]
    columns = lax.all_to_all(hidden_in, "seq", split_axis=1, concat_axis=0, tiled=True)

    def term(start, count):
        block = lax.dynamic_slice_in_dim(columns, start, count, 0)
        return jnp.concatenate(
            [
                jnp.dot(block, gate_proj, preferred_element_type=jnp.float32),
                jnp.dot(block, up_proj, preferred_element_type=jnp.float32),
            ],
            axis=1,
        )

    joined = summed_rows(term, length, "seq")
    gate = joined[:, :width]
    up = joined[:, width:]
    hidden = (jax.nn.gelu(gate, approximate=True) * up).astype(jnp.bfloat16)
    output = channel_total(jnp.dot(hidden, down_proj, preferred_element_type=jnp.float32))
    return (middle.astype(jnp.float32) + output).astype(jnp.bfloat16)


def solution(mesh):
    in_specs = (
        P("seq", None),
        P(),
        P(None, "tp"),
        P(None, "tp"),
        P(None, "tp"),
        P("tp"),
        P("tp", None, None),
        P("tp"),
        P("tp", None, None),
        P("tp"),
        P("tp"),
        P("tp", None),
        P(),
        P("seq", "tp"),
        P("seq", "tp"),
        P("tp", None),
    )
    out_specs = P("seq", None)
    return jax.shard_map(
        on_device, mesh=mesh, in_specs=in_specs, out_specs=out_specs, check_vma=False
    )
```

profile of v0, /device:TPU:0, one launch (start us, length us, event | category | flops | bytes accessed | tf_op | source)
XLA Modules:
  0.0 391.7 jit_solution(13531175450782179382)
XLA Ops:
  8.8 4.1 %convolution_convert_fusion.4 = bf16[256,512]{1,0:T(8,128)(2,1)S(1)} fusion(bf16[4096,512]{1,0:T(8,128)(2,1)} %param.20, bf16[256,4096]{1,0:T(8,128)(2,1)} %param.18, f32[4096]{0:T(1024)} %param.19, f32[256]{0:T(256)S(1)} %add_rsqrt_fusion.1), kind=kOutput, calls=%fused_computation.33 | convolution fusion | flops 1078067200 | bytes 6571008 | tf_op jit(solution)/shard_map/dot_general | solution.py:94
  13.0 4.9 %collective-permute-start = (bf16[3,512]{1,0:T(4,128)(2,1)S(1)}, bf16[3,512]{1,0:T(4,128)(2,1)S(1)}, u32[]{:S(2)}, u32[]{:S(2)}) collective-permute-start(bf16[3,512]{1,0:T(4,128)(2,1)S(1)} %slice.356), channel_id=1, source_target_pairs={{0,1},{1,2},{2,3},{4,5},{5,6},{6,7},{8,9},{9,10},{10,11},{12,13},{... | collective-permute-start | bytes 9224 | tf_op jit(solution)/shard_map/ppermute | solution.py:12
  26.8 2.6 select_multiply_fusion
  30.2 2.5 slice.336
  35.2 2.5 slice.281
  38.4 2.5 slice.284
  40.9 2.5 slice.280
  43.4 2.5 slice.279
  90.1 2.6 pad.128
  94.4 2.6 pad.112
  97.0 2.6 pad.113
  100.4 9.7 %all-gather.1 = f32[4,1,512]{2,1,0:T(1,128)S(1)} all-gather(f32[1,1,512]{2,1,0:T(1,128)S(1)} %add_bitcast_fusion), channel_id=1, replica_groups=mesh['tp'=8,'seq'=4] {'seq'}, dimensions={0}, use_global_device_ids=true | all-gather | bytes 10240 | tf_op jit(solution)/shard_map/all_gather | solution.py:17
  112.4 7.1 %all-gather = f32[4,1,512]{2,1,0:T(1,128)S(1)} all-gather(f32[1,1,512]{2,1,0:T(1,128)S(1)} %add_bitcast_fusion.1), channel_id=1, replica_groups=mesh['tp'=8,'seq'=4] {'seq'}, dimensions={0}, use_global_device_ids=true | all-gather | bytes 10240 | tf_op jit(solution)/shard_map/all_gather | solution.py:17
  119.8 8.6 %convolution_convert_fusion.1 = bf16[256,4096]{1,0:T(8,128)(2,1)} fusion(bf16[512,4096]{1,0:T(8,128)(2,1)} %param.29, bf16[4096,512]{1,0:T(8,128)(2,1)} %param.21, bf16[256,4096]{1,0:T(8,128)(2,1)} %param.18, f32[4096]{0:T(1024)S(1)} %copy-done.18, f32[256]{0:T(256)S(1)} %copy-done.16, f32[256,512]{1,0:T(8,128)} %pad.128, f32[256,512]{1,0:T(8,128)} %pad.129, ...), kind=kOutput, calls=%fused_computation.11 | convolution fusion | flops 2154561536 | bytes 14699520 | tf_op jit(solution)/shard_map/dot_general | solution.py:117
  128.5 65.4 %all-reduce.35.cloned.1.call-done = bf16[256,4096]{1,0:T(8,128)(2,1)} async-done(((bf16[256,4096]{1,0:T(8,128)(2,1)}), bf16[256,4096]{1,0:T(8,128)(2,1)}) %all-reduce.35.cloned.1.call-update) | async-done | bytes 2097168 | tf_op jit(solution)/shard_map/psum | solution.py:67
  193.9 3.0 fusion.3
  198.4 27.5 %all_to_all.19 = bf16[256,4,1024]{2,0,1:T(8,128)(2,1)S(1)} all-to-all(bf16[256,4,1024]{2,0,1:T(8,128)(2,1)S(1)} %bitcast.50), channel_id=1, replica_groups=mesh['tp'=8,'seq'=4] {'seq'}, dimensions={1} | all-to-all | bytes 4194304 | tf_op jit(solution)/shard_map/all_to_all | solution.py:121
  225.9 3.6 convolution_convert_fusion.2
  229.5 3.6 convolution_convert_fusion.3
  233.2 3.6 pad_maximum_fusion
  236.8 67.6 %reduce-scatter.2.cloned.1.call-done = bf16[256,3072]{1,0:T(8,128)(2,1)} async-done(((bf16[1024,3072]{1,0:T(8,128)(2,1)}), bf16[256,3072]{1,0:T(8,128)(2,1)}) %reduce-scatter.2.cloned.1.call-update) | async-done | bytes 1572880 | tf_op jit(solution)/shard_map/reduce_scatter | solution.py:35
  306.2 9.4 %convolution_convert_fusion = bf16[256,4096]{1,0:T(8,128)(2,1)} fusion(bf16[1536,4096]{1,0:T(8,128)(2,1)} %param.33, f32[256,3072]{1,0:T(8,128)S(1)} %convert_element_type.66), kind=kOutput, calls=%fused_computation.10 | convolution fusion | flops 3226206208 | bytes 17825792 | tf_op jit(solution)/shard_map/dot_general | solution.py:137
  315.7 65.1 %all-reduce.37.cloned.1.call-done = bf16[256,4096]{1,0:T(8,128)(2,1)} async-done(((bf16[256,4096]{1,0:T(8,128)(2,1)}), bf16[256,4096]{1,0:T(8,128)(2,1)}) %all-reduce.37.cloned.1.call-update) | async-done | bytes 2097168 | tf_op jit(solution)/shard_map/psum | solution.py:67
  380.8 4.3 %fusion.7 = bf16[256,4096]{1,0:T(8,128)(2,1)} fusion(bf16[256,4096]{1,0:T(8,128)(2,1)} %copy-done.2, bf16[256,4096]{1,0:T(8,128)(2,1)} %all-reduce.37.cloned.1.call-done), kind=kLoop, calls=%fused_computation.19 | loop fusion | flops 4194304 | bytes 6291456 | tf_op jit(solution)/shard_map/convert_element_type | solution.py:138
  (189 shorter events, 67.5 us)
Async XLA Ops:
  6.5 219.4 %copy-start = (bf16[1024,1536]{1,0:T(8,128)(2,1)S(1)}, bf16[1024,1536]{1,0:T(8,128)(2,1)}, u32[]{:S(2)}) copy-start(bf16[1024,1536]{1,0:T(8,128)(2,1)} %param.32) | copy-start | bytes 9437188
  6.5 187.3 %all-reduce.35.cloned.1.call-start = ((), (), s32[]{:S(2)}) async-start(), calls=%async_computation.2 | async-start | bytes 4194304 | tf_op jit(solution)/shard_map/psum | solution.py:67
  8.8 4.2 %copy-start.15 = (f32[256]{0:T(256)}, f32[256]{0:T(256)S(1)}, u32[]{:S(2)}) copy-start(f32[256]{0:T(256)S(1)} %add_rsqrt_fusion.1) | copy-start | bytes 3076
  8.8 9.1 %copy-start.13 = (f32[512]{0:T(512)S(1)}, f32[512]{0:T(512)}, u32[]{:S(2)}) copy-start(f32[512]{0:T(512)} %param.28) | copy-start | bytes 6148
  8.8 9.1 %copy-start.10 = (f32[4,512]{1,0:T(4,128)S(1)}, f32[4,512]{1,0:T(4,128)}, u32[]{:S(2)}) copy-start(f32[4,512]{1,0:T(4,128)} %param.22) | copy-start | bytes 24580
  8.8 10.5 %copy-start.14 = (f32[512]{0:T(512)S(1)}, f32[512]{0:T(512)}, u32[]{:S(2)}) copy-start(f32[512]{0:T(512)} %param.23) | copy-start | bytes 6148
  13.0 6.2 %collective-permute-start = (bf16[3,512]{1,0:T(4,128)(2,1)S(1)}, bf16[3,512]{1,0:T(4,128)(2,1)S(1)}, u32[]{:S(2)}, u32[]{:S(2)}) collective-permute-start(bf16[3,512]{1,0:T(4,128)(2,1)S(1)} %slice.356), channel_id=1, source_target_pairs={{0,1},{1,2},{2,3},{4,5},{5,6},{6,7},{8,9},{9,10},{10,11},{12,13},{... | collective-permute-start | bytes 9224 | tf_op jit(solution)/shard_map/ppermute | solution.py:12
  18.0 1.6 copy-start.6
  19.3 7.5 %copy-start.11 = (f32[512]{0:T(512)S(1)}, f32[512]{0:T(512)}, u32[]{:S(2)}) copy-start(f32[512]{0:T(512)} %param.25) | copy-start | bytes 6148
  19.3 7.5 %copy-start.12 = (f32[512]{0:T(512)S(1)}, f32[512]{0:T(512)}, u32[]{:S(2)}) copy-start(f32[512]{0:T(512)} %param.27) | copy-start | bytes 6148
  29.4 0.8 copy-start.3
  47.2 0.7 copy-start.4
  58.5 8.2 %copy-start.7 = (f32[31,512]{1,0:T(8,128)S(1)}, f32[31,512]{1,0:T(8,128)}, u32[]{:S(2)}) copy-start(f32[31,512]{1,0:T(8,128)} %slice.332) | copy-start | bytes 190468
  58.5 8.2 %copy-start.8 = (f32[31,512]{1,0:T(8,128)S(1)}, f32[31,512]{1,0:T(8,128)}, u32[]{:S(2)}) copy-start(f32[31,512]{1,0:T(8,128)} %slice.291) | copy-start | bytes 190468
  87.2 32.5 %copy-start.16 = (f32[256]{0:T(256)S(1)}, f32[256]{0:T(256)}, u32[]{:S(2)}) copy-start(f32[256]{0:T(256)} %copy-done.15) | copy-start | bytes 3076
  87.2 32.5 %copy-start.18 = (f32[4096]{0:T(1024)S(1)}, f32[4096]{0:T(1024)}, u32[]{:S(2)}) copy-start(f32[4096]{0:T(1024)} %param.19) | copy-start | bytes 49156
  89.4 20.7 %copy-start.5 = (f32[128,512]{1,0:T(8,128)S(1)}, f32[128,512]{1,0:T(8,128)}, u32[]{:S(2)}) copy-start(f32[128,512]{1,0:T(8,128)} %add.317) | copy-start | bytes 786436
  128.4 69.0 %copy-start.9 = (f32[4096]{0:T(1024)S(1)}, f32[4096]{0:T(1024)}, u32[]{:S(2)}) copy-start(f32[4096]{0:T(1024)} %param.30) | copy-start | bytes 49156
  128.4 176.0 %reduce-scatter.2.cloned.1.call-start = ((), (), s32[]{:S(2)}) async-start(), calls=%async_computation.3 | async-start | bytes 7864320 | tf_op jit(solution)/shard_map/reduce_scatter | solution.py:35
  196.9 1.3 copy-start.2
  225.9 3.6 copy-start.17
  236.8 144.0 %all-reduce.37.cloned.1.call-start = ((), (), s32[]{:S(2)}) async-start(), calls=%async_computation.4 | async-start | bytes 4194304 | tf_op jit(solution)/shard_map/psum | solution.py:67
  315.6 69.5 %copy-start.1 = (bf16[1024,1536]{1,0:T(8,128)(2,1)S(1)}, bf16[1024,1536]{1,0:T(8,128)(2,1)}, u32[]{:S(2)}) copy-start(bf16[1024,1536]{1,0:T(8,128)(2,1)} %param.32) | copy-start | bytes 9437188
Sparse Core Ops, SparseCore 0:
  128.5 65.2 all-reduce.34
  236.9 67.4 reduce-scatter.1
  315.8 64.9 all-reduce.36
where the time goes:
time: 393 us; the launch traced here: 392 us
  waiting for transfers between devices  199 us (51%)
  local copies, waits for them, and re-layouts  53.7 us (14%)
  blocking collectives  44.2 us (11%)
  other arithmetic  43 us (11%)
  matrix products  32.6 us (8%)
  between operations  13.7 us (3%)
  starting transfers between devices  4.99 us (1%)
    psum x2, waiting for transfers between devices, channel_total(): lax.psum(partial_value.astype(jnp.bfloat16), 'tp').astype(jnp.float32)  131 us
    reduce_scatter x1, waiting for transfers between devices, summed_rows(): lax.psum_scatter(everything.astype(jnp.bfloat16), axis, scatter_dimension...  67.6 us
    slice x52, local copies, waits for them, and re-layouts, on_device(): lax.associative_scan(combine_state, (decay, pushed), axis=0)  28 us
    all_to_all x1, blocking collectives, on_device(): lax.all_to_all(hidden_in, 'seq', split_axis=1, concat_axis=0, tiled=True)  27.5 us
    pad x28, local copies, waits for them, and re-layouts, on_device(): lax.associative_scan(combine_state, (decay, pushed), axis=0)  19.7 us
    all_gather x2, blocking collectives, carried_in(): everything = jax.tree.map(lambda part: lax.all_gather(part, axis), shard)  16.7 us
    dot_general x1, matrix products, on_device(): jnp.dot(hidden, down_proj, preferred_element_type=jnp.float32)  9.43 us
    dot_general x1, matrix products, on_device(): jnp.dot(gated, out_proj, preferred_element_type=jnp.float32)  8.63 us
  transfers between devices with their start and end apart: 4, of which 4 were waited for; matrix products, arithmetic and copies ran while one was open for 0% of the time, Pallas kernels for 0%

commit v1 on v0

v1 whole, which is shorter than its diff:
```python
import functools

import jax
import jax.numpy as jnp
from jax import lax
from jax.experimental import pallas as pl
from jax.experimental.pallas import tpu as pltpu
from jax.sharding import PartitionSpec as P

epsilon = 1e-06
LOGICAL = pl.DeviceIdType.MESH
LANES = 128
EDGE = 16


def greet(axis, peers):
    barrier = pltpu.get_barrier_semaphore()
    for peer in peers:
        pl.semaphore_signal(barrier, inc=1, device_id={axis: peer}, device_id_type=LOGICAL)
    pl.semaphore_wait(barrier, len(peers))


def one_minus_exp(x):
    series = 1.0 + x * (1.0 / 9.0)
    for k in range(8, 1, -1):
        series = 1.0 + x * (1.0 / k) * series
    return jnp.where(x > -0.5, -x * series, 1.0 - jnp.exp(x))


def recurrence_kernel(
    count,
    taps,
    inner_ref,
    branch_ref,
    conv_weight_ref,
    conv_bias_ref,
    input_gate_ref,
    input_bias_ref,
    decay_gate_ref,
    decay_bias_ref,
    slope_ref,
    gated_ref,
    tail_ref,
    decays_ref,
    states_ref,
    ends_ref,
    arrived_ref,
    tail_send,
    tail_recv,
    end_send,
    end_recv,
):
    me = lax.axis_index("seq")
    length, channels = inner_ref.shape
    heads, head = input_gate_ref.shape[0], input_gate_ref.shape[1]
    peers = [lax.rem(me + offset, count) for offset in range(1, count)]
    greet("seq", peers)
    tail_copy = pltpu.make_async_remote_copy(
        src_ref=inner_ref.at[pl.ds(length - EDGE, EDGE), :],
        dst_ref=tail_ref,
        send_sem=tail_send,
        recv_sem=tail_recv,
        device_id={"seq": lax.rem(me + 1, count)},
        device_id_type=LOGICAL,
    )
    tail_copy.start()
    tail_copy.wait()
    follows = jnp.where(me > 0, 1.0, 0.0)

    for h in range(heads):
        columns = pl.ds(h * head, head)
        row = lax.broadcasted_iota(jnp.int32, (length, head), 0)
        current = inner_ref[:, columns].astype(jnp.float32)
        tail = tail_ref[:, columns].astype(jnp.float32) * follows
        before = jnp.concatenate([tail, jnp.zeros((length - EDGE, head), jnp.float32)], axis=0)
        total = conv_bias_ref[:, columns] + conv_weight_ref[0:1, columns] * current
        for tap in range(1, taps):
            shifted = jnp.where(
                row < tap,
                pltpu.roll(before, length + tap - EDGE, 0),
                pltpu.roll(current, tap, 0),
            )
            total = total + conv_weight_ref[tap : tap + 1, columns] * shifted
        smoothed = total.astype(jnp.bfloat16)
        input_rate = jax.nn.sigmoid(
            jnp.dot(smoothed, input_gate_ref[h], preferred_element_type=jnp.float32)
            + input_bias_ref[:, columns]
        )
        decay_rate = jax.nn.sigmoid(
            jnp.dot(smoothed, decay_gate_ref[h], preferred_element_type=jnp.float32)
            + decay_bias_ref[:, columns]
        )
        log_decay = decay_rate * slope_ref[:, columns]
        scale_in = jnp.sqrt(one_minus_exp(2.0 * log_decay))
        scale_in = jnp.where(jnp.logical_and(row == 0, me == 0), 1.0, scale_in)
        decays_ref[:, columns] = jnp.exp(log_decay)
        states_ref[:, columns] = smoothed.astype(jnp.float32) * input_rate * scale_in

    for c in range(channels // LANES):
        columns = pl.ds(c * LANES, LANES)
        row = lax.broadcasted_iota(jnp.int32, (length, LANES), 0)
        decay, state = decays_ref[:, columns], states_ref[:, columns]
        step = 1
        while step < length:
            reached = row >= step
            state = state + decay * jnp.where(reached, pltpu.roll(state, step, 0), 0.0)
            decay = decay * jnp.where(reached, pltpu.roll(decay, step, 0), 1.0)
            step *= 2
        decays_ref[:, columns] = decay
        states_ref[:, columns] = state
        ends_ref[0:1, columns] = decay[length - 1 :, :]
        ends_ref[1:2, columns] = state[length - 1 :, :]

    copies = [
        pltpu.make_async_remote_copy(
            src_ref=ends_ref,
            dst_ref=arrived_ref.at[k],
            send_sem=end_send.at[k],
            recv_sem=end_recv.at[k],
            device_id={"seq": peers[k]},
            device_id_type=LOGICAL,
        )
        for k in range(count - 1)
    ]
    for copy in copies:
        copy.start()
    for copy in copies:
        copy.wait()
    carried = jnp.zeros((1, channels), jnp.float32)
    for k in range(count - 2, -1, -1):
        new = arrived_ref[k, 0:1, :] * carried + arrived_ref[k, 1:2, :]
        carried = jnp.where(me >= k + 1, new, carried)
    gated_ref[...] = (
        (states_ref[...] + decays_ref[...] * carried) * branch_ref[...]
    ).astype(jnp.bfloat16)


def recurrence(inner, branch, conv_weight, conv_bias, input_gate, input_bias, decay_gate, decay_bias, slope):
    count = lax.axis_size("seq")
    length, channels = inner.shape
    vmem = pl.BlockSpec(memory_space=pltpu.VMEM)
    return pl.pallas_call(
        functools.partial(recurrence_kernel, count, conv_weight.shape[0]),
        out_shape=jax.ShapeDtypeStruct((length, channels), jnp.bfloat16),
        in_specs=[vmem] * 9,
        out_specs=vmem,
        scratch_shapes=[
            pltpu.VMEM((EDGE, channels), jnp.bfloat16),
            pltpu.VMEM((length, channels), jnp.float32),
            pltpu.VMEM((length, channels), jnp.float32),
            pltpu.VMEM((8, channels), jnp.float32),
            pltpu.VMEM((count - 1, 8, channels), jnp.float32),
            pltpu.SemaphoreType.DMA,
            pltpu.SemaphoreType.DMA,
            pltpu.SemaphoreType.DMA((count - 1,)),
            pltpu.SemaphoreType.DMA((count - 1,)),
        ],
        compiler_params=pltpu.CompilerParams(
            collective_id=0, has_side_effects=True, vmem_limit_bytes=24 * 2**20
        ),
    )(
        inner,
        branch,
        conv_weight,
        conv_bias[None],
        input_gate,
        input_bias[None],
        decay_gate,
        decay_bias[None],
        slope[None],
    )


def summed_rows(product, extent, axis):
    everything = product(jnp.int32(0), lax.axis_size(axis) * extent)
    own = lax.psum_scatter(everything.astype(jnp.bfloat16), axis, scatter_dimension=0, tiled=True)
    return own.astype(jnp.float32)


def rms_norm(values, gain):
    wide = values.astype(jnp.float32)
    factor = lax.rsqrt(jnp.mean(wide * wide, axis=-1, keepdims=True) + epsilon)
    return (wide * factor * gain).astype(jnp.bfloat16)


def channel_total(partial_value):
    return lax.psum(partial_value.astype(jnp.bfloat16), "tp").astype(jnp.float32)


def on_device(
    residual,
    mix_gain,
    in_proj,
    branch_proj,
    conv_weight,
    conv_bias,
    input_gate,
    input_bias,
    decay_gate,
    decay_bias,
    decay_param,
    out_proj,
    mlp_gain,
    gate_proj,
    up_proj,
    down_proj,
):
    length = residual.shape[0]
    normed = rms_norm(residual, mix_gain)
    branch = jax.nn.gelu(
        jnp.dot(normed, branch_proj, preferred_element_type=jnp.float32), approximate=True
    )
    inner = jnp.dot(normed, in_proj, preferred_element_type=jnp.float32).astype(jnp.bfloat16)
    gated = recurrence(
        inner,
        branch,
        conv_weight,
        conv_bias,
        input_gate,
        input_bias,
        decay_gate,
        decay_bias,
        -8.0 * jax.nn.softplus(decay_param),
    )
    mixed = channel_total(jnp.dot(gated, out_proj, preferred_element_type=jnp.float32))
    middle = lax.optimization_barrier((residual.astype(jnp.float32) + mixed).astype(jnp.bfloat16))
    hidden_in = rms_norm(middle, mlp_gain)
    width = gate_proj.shape[1]
    columns = lax.all_to_all(hidden_in, "seq", split_axis=1, concat_axis=0, tiled=True)

    def term(start, count):
        block = lax.dynamic_slice_in_dim(columns, start, count, 0)
        return jnp.concatenate(
            [
                jnp.dot(block, gate_proj, preferred_element_type=jnp.float32),
                jnp.dot(block, up_proj, preferred_element_type=jnp.float32),
            ],
            axis=1,
        )

    joined = summed_rows(term, length, "seq")
    gate = joined[:, :width]
    up = joined[:, width:]
    hidden = (jax.nn.gelu(gate, approximate=True) * up).astype(jnp.bfloat16)
    output = channel_total(jnp.dot(hidden, down_proj, preferred_element_type=jnp.float32))
    return (middle.astype(jnp.float32) + output).astype(jnp.bfloat16)


def solution(mesh):
    in_specs = (
        P("seq", None),
        P(),
        P(None, "tp"),
        P(None, "tp"),
        P(None, "tp"),
        P("tp"),
        P("tp", None, None),
        P("tp"),
        P("tp", None, None),
        P("tp"),
        P("tp"),
        P("tp", None),
        P(),
        P("seq", "tp"),
        P("seq", "tp"),
        P("tp", None),
    )
    out_specs = P("seq", None)
    return jax.shard_map(
        on_device, mesh=mesh, in_specs=in_specs, out_specs=out_specs, check_vma=False
    )
```

time: 393 us -> 294 us (0.75)
  local copies, waits for them, and re-layouts: 53.7 us -> 0.7 us
  other arithmetic: 43 us -> 16.9 us
  blocking collectives: 44.2 us -> 27.5 us
  Pallas kernels: 0 us -> 11.8 us
  matrix products: 32.6 us -> 25 us
  starting transfers between devices: 4.99 us -> 0.27 us
    slice x54 -> x0, local copies, waits for them, and re-layouts: 28 us -> none  [the longest x52 28 us: on_device(): lax.associative_scan(combine_state, (decay, pushed), axis=0)]
    pad x28 -> x0, local copies, waits for them, and re-layouts: 19.7 us -> none  [on_device(): lax.associative_scan(combine_state, (decay, pushed), axis=0)]
    all_gather x2 -> x0, blocking collectives: 16.7 us -> none  [carried_in(): everything = jax.tree.map(lambda part: lax.all_gather(part, axis), shard)]
    add x26 -> x0, other arithmetic: 15.3 us -> none  [the longest x13 7.72 us: combine_state(): return (earlier[0] * later[0], later[0] * earlier[1] + later[1])]
    pallas_call x0 -> x1, Pallas kernels: none -> 11.8 us  [recurrence(): pl.pallas_call(functools.partial(recurrence_kernel, count, conv_weight.sh...]
    concatenate x13 -> x0, other arithmetic: 6.95 us -> none  [on_device(): lax.associative_scan(combine_state, (decay, pushed), axis=0)]
    dot_general x1, matrix products: 8.63 us -> 2.58 us  [on_device(): jnp.dot(gated, out_proj, preferred_element_type=jnp.float32)]
    ppermute x1 -> x0, starting transfers between devices: 4.9 us -> none  [from_behind(): lax.ppermute(value, axis, [(source, source + steps) for source in range(l...]
  transfers between devices with their start and end apart: 4 -> 3, of which waited for: 4 -> 3; matrix products, arithmetic and copies ran while one was open for 0% -> 0% of each run, Pallas kernels for 0% -> 0%
where the time goes in v1:
time: 294 us; the launch traced here: 293 us
  waiting for transfers between devices  198 us (67%)
  blocking collectives  27.5 us (9%)
  matrix products  25 us (9%)
  other arithmetic  16.9 us (6%)
  between operations  13.3 us (5%)
  Pallas kernels  11.8 us (4%)
    psum x2, waiting for transfers between devices, channel_total(): lax.psum(partial_value.astype(jnp.bfloat16), 'tp').astype(jnp.float32)  131 us
    reduce_scatter x1, waiting for transfers between devices, summed_rows(): lax.psum_scatter(everything.astype(jnp.bfloat16), axis, scatter_dimension...  67.4 us
    all_to_all x1, blocking collectives, on_device(): lax.all_to_all(hidden_in, 'seq', split_axis=1, concat_axis=0, tiled=True)  27.5 us
    pallas_call x1, Pallas kernels, recurrence(): pl.pallas_call(functools.partial(recurrence_kernel, count, conv_weight.sh...  11.8 us
    dot_general x1, matrix products, on_device(): jnp.dot(hidden, down_proj, preferred_element_type=jnp.float32)  9.45 us
  transfers between devices with their start and end apart: 3, of which 3 were waited for; matrix products, arithmetic and copies ran while one was open for 0% of the time, Pallas kernels for 0%

profile of v1, /device:TPU:0, one launch (start us, length us, event | category | flops | bytes accessed | tf_op | source)
XLA Modules:
  0.0 293.4 jit_solution(16779114175655108544)
XLA Ops:
  6.5 2.2 fusion
  8.8 0.7 fusion.34
  9.5 4.3 %convolution_convert_fusion.4.inner_ref = bf16[256,512]{1,0:T(8,128)(2,1)S(1)} fusion(bf16[4096,512]{1,0:T(8,128)(2,1)} %param.18, bf16[256,4096]{1,0:T(8,128)(2,1)} %param.16, f32[4096]{0:T(1024)} %param.17, f32[256]{0:T(256)S(1)} %add_rsqrt_fusion.1), kind=kOutput, calls=%fused_computation.30 | convolution fusion | flops 1078067200 | bytes 6571008 | tf_op jit(solution)/shard_map/dot_general | solution.py:213
  13.8 0.4 copy-done.11
  14.2 1.4 fusion.31.branch_ref
  15.7 11.8 %shard_map.154 = bf16[256,512]{1,0:T(8,128)(2,1)S(1)} custom-call(bf16[256,512]{1,0:T(8,128)(2,1)S(1)} %convolution_convert_fusion.4.inner_ref, f32[256,512]{1,0:T(8,128)S(1)} %fusion.31.branch_ref, f32[4,512]{1,0:T(4,128)S(1)} %copy-done.4, f32[1,512]{1,0:T(1,128)S(1)} %bitcast.21, bf16[2,256,256]{2,1,0:T(8,128)(2,1)S(1)} %copy-done.2, ...), custom_call_target="tpu_custom_call" | custom-call | tf_op jit(solution)/shard_map/pallas_call | solution.py:142
  27.5 2.6 convolution_convert_fusion.1
  30.2 0.0 reduce-scatter.2.cloned.1.call-start
  30.2 65.3 %all-reduce.3.cloned.1.call-done = bf16[256,4096]{1,0:T(8,128)(2,1)} async-done(((bf16[256,4096]{1,0:T(8,128)(2,1)}), bf16[256,4096]{1,0:T(8,128)(2,1)}) %all-reduce.3.cloned.1.call-update) | async-done | bytes 2097168 | tf_op jit(solution)/shard_map/psum | solution.py:187
  95.5 3.0 %fusion.3 = bf16[256,4096]{1,0:T(8,128)(2,1)S(1)} fusion(bf16[256,4096]{1,0:T(8,128)(2,1)} %param.16, bf16[256,4096]{1,0:T(8,128)(2,1)} %all-reduce.3.cloned.1.call-done), kind=kLoop, calls=%fused_computation.12 | loop fusion | flops 4194304 | bytes 6291456 | tf_op jit(solution)/shard_map/convert_element_type | solution.py:226
  98.6 0.5 fusion.4
  99.1 0.7 fusion.6
  99.8 0.0 copy-done.8
  99.9 0.2 copy.20
  100.1 27.5 %all_to_all.19 = bf16[256,4,1024]{2,0,1:T(8,128)(2,1)S(1)} all-to-all(bf16[256,4,1024]{2,0,1:T(8,128)(2,1)S(1)} %bitcast.25), channel_id=1, replica_groups=mesh['tp'=8,'seq'=4] {'seq'}, dimensions={1} | all-to-all | bytes 4194304 | tf_op jit(solution)/shard_map/all_to_all | solution.py:229
  127.6 3.6 %convolution_convert_fusion.2 = bf16[1024,1536]{1,0:T(8,128)(2,1)S(1)} fusion(bf16[1024,1024]{1,0:T(8,128)(2,1)S(1)} %bitcast.26, bf16[1024,1536]{1,0:T(8,128)(2,1)S(1)} %copy-done), kind=kOutput, calls=%fused_computation.17 | convolution fusion | flops 3222798336 | bytes 8388608 | tf_op jit(solution)/shard_map/dot_general | solution.py:236
  131.2 3.6 %convolution_convert_fusion.3 = bf16[1024,1536]{1,0:T(8,128)(2,1)S(1)} fusion(bf16[1024,1024]{1,0:T(8,128)(2,1)S(1)} %bitcast.27, bf16[1024,1536]{1,0:T(8,128)(2,1)S(1)} %copy-done.13), kind=kOutput, calls=%fused_computation.18 | convolution fusion | flops 3222798336 | bytes 8388608 | tf_op jit(solution)/shard_map/dot_general | solution.py:235
  134.8 3.6 %pad_maximum_fusion = bf16[1024,3072]{1,0:T(8,128)(2,1)} fusion(bf16[1024,1536]{1,0:T(8,128)(2,1)S(1)} %convolution_convert_fusion.2, bf16[1024,1536]{1,0:T(8,128)(2,1)S(1)} %convolution_convert_fusion.3), kind=kLoop, calls=%fused_computation | loop fusion | flops 12582912 | bytes 12582912 | tf_op jit(solution)/shard_map/concatenate | solution.py:233
  138.5 0.2 all-reduce.5.cloned.1.call-start
  138.7 67.4 %reduce-scatter.2.cloned.1.call-done = bf16[256,3072]{1,0:T(8,128)(2,1)} async-done(((bf16[1024,3072]{1,0:T(8,128)(2,1)}), bf16[256,3072]{1,0:T(8,128)(2,1)}) %reduce-scatter.2.cloned.1.call-update) | async-done | bytes 1572880 | tf_op jit(solution)/shard_map/reduce_scatter | solution.py:176
  206.1 1.8 convert_element_type.50
  207.9 9.4 %convolution_convert_fusion = bf16[256,4096]{1,0:T(8,128)(2,1)} fusion(bf16[1536,4096]{1,0:T(8,128)(2,1)} %param.31, f32[256,3072]{1,0:T(8,128)S(1)} %convert_element_type.50), kind=kOutput, calls=%fused_computation.7 | convolution fusion | flops 3226206208 | bytes 17825792 | tf_op jit(solution)/shard_map/dot_general | solution.py:245
  217.4 65.2 %all-reduce.5.cloned.1.call-done = bf16[256,4096]{1,0:T(8,128)(2,1)} async-done(((bf16[256,4096]{1,0:T(8,128)(2,1)}), bf16[256,4096]{1,0:T(8,128)(2,1)}) %all-reduce.5.cloned.1.call-update) | async-done | bytes 2097168 | tf_op jit(solution)/shard_map/psum | solution.py:187
  282.6 4.3 %fusion.7 = bf16[256,4096]{1,0:T(8,128)(2,1)} fusion(bf16[256,4096]{1,0:T(8,128)(2,1)} %copy-done.8, bf16[256,4096]{1,0:T(8,128)(2,1)} %all-reduce.5.cloned.1.call-done), kind=kLoop, calls=%fused_computation.16 | loop fusion | flops 4194304 | bytes 6291456 | tf_op jit(solution)/shard_map/convert_element_type | solution.py:246
  (34 shorter events, 0.1 us)
Async XLA Ops:
  6.5 121.0 %copy-start = (bf16[1024,1536]{1,0:T(8,128)(2,1)S(1)}, bf16[1024,1536]{1,0:T(8,128)(2,1)}, u32[]{:S(2)}) copy-start(bf16[1024,1536]{1,0:T(8,128)(2,1)} %param.30) | copy-start | bytes 9437188
  6.5 89.0 %all-reduce.3.cloned.1.call-start = ((), (), s32[]{:S(2)}) async-start(), calls=%async_computation.2 | async-start | bytes 4194304 | tf_op jit(solution)/shard_map/psum | solution.py:187
  9.5 4.3 %copy-start.9 = (bf16[256,4096]{1,0:T(8,128)(2,1)S(1)}, bf16[256,4096]{1,0:T(8,128)(2,1)}, u32[]{:S(2)}) copy-start(bf16[256,4096]{1,0:T(8,128)(2,1)} %param.16) | copy-start | bytes 6291460
  9.5 4.7 %copy-start.11 = (bf16[4096,512]{1,0:T(8,128)(2,1)S(1)}, bf16[4096,512]{1,0:T(8,128)(2,1)}, u32[]{:S(2)}) copy-start(bf16[4096,512]{1,0:T(8,128)(2,1)} %param.19) | copy-start | bytes 12582916
  9.5 4.7 %copy-start.14 = (f32[4096]{0:T(1024)S(1)}, f32[4096]{0:T(1024)}, u32[]{:S(2)}) copy-start(f32[4096]{0:T(1024)} %param.17) | copy-start | bytes 49156
  14.2 1.5 copy-start.2
  14.2 1.5 copy-start.3
  14.2 1.5 copy-start.4
  14.2 1.5 copy-start.5
  14.2 1.5 copy-start.6
  14.2 1.5 copy-start.7
  14.2 13.3 %copy-start.12 = (bf16[512,4096]{1,0:T(8,128)(2,1)S(1)}, bf16[512,4096]{1,0:T(8,128)(2,1)}, u32[]{:S(2)}) copy-start(bf16[512,4096]{1,0:T(8,128)(2,1)} %param.27) | copy-start | bytes 12582916
  30.1 68.9 %copy-start.10 = (f32[4096]{0:T(1024)S(1)}, f32[4096]{0:T(1024)}, u32[]{:S(2)}) copy-start(f32[4096]{0:T(1024)} %param.28) | copy-start | bytes 49156
  30.2 176.0 %reduce-scatter.2.cloned.1.call-start = ((), (), s32[]{:S(2)}) async-start(), calls=%async_computation.3 | async-start | bytes 7864320 | tf_op jit(solution)/shard_map/reduce_scatter | solution.py:176
  98.5 1.3 copy-start.8
  127.6 3.6 %copy-start.13 = (bf16[1024,1536]{1,0:T(8,128)(2,1)S(1)}, bf16[1024,1536]{1,0:T(8,128)(2,1)}, u32[]{:S(2)}) copy-start(bf16[1024,1536]{1,0:T(8,128)(2,1)} %param.29) | copy-start | bytes 9437188
  138.5 144.1 %all-reduce.5.cloned.1.call-start = ((), (), s32[]{:S(2)}) async-start(), calls=%async_computation.4 | async-start | bytes 4194304 | tf_op jit(solution)/shard_map/psum | solution.py:187
  217.4 69.5 %copy-start.1 = (bf16[1024,1536]{1,0:T(8,128)(2,1)S(1)}, bf16[1024,1536]{1,0:T(8,128)(2,1)}, u32[]{:S(2)}) copy-start(bf16[1024,1536]{1,0:T(8,128)(2,1)} %param.30) | copy-start | bytes 9437188
Sparse Core Ops, SparseCore 0:
  30.3 65.2 all-reduce.2
  138.6 67.4 reduce-scatter.1
  217.5 65.0 all-reduce.4

commit v2 on v1

--- a/solution.py
+++ b/solution.py
@@ -11,6 +11,8 @@
 LOGICAL = pl.DeviceIdType.MESH
 LANES = 128
 EDGE = 16
+HEIGHT = 16
+LAG = 4
 
 
 def greet(axis, peers):
@@ -183,8 +185,145 @@
     return (wide * factor * gain).astype(jnp.bfloat16)
 
 
-def channel_total(partial_value):
-    return lax.psum(partial_value.astype(jnp.bfloat16), "tp").astype(jnp.float32)
+def summed_kernel(
+    chips,
+    part_ref,
+    base_ref,
+    out_ref,
+    pair_ref,
+    stage_ref,
+    left_ref,
+    right_ref,
+    pair_send,
+    pair_recv,
+    line_send,
+    left_recv,
+    right_recv,
+    out_send,
+    out_recv,
+    share_send,
+    share_recv,
+):
+    me = lax.axis_index("tp")
+    core, chip = lax.rem(me, 2), lax.div(me, 2)
+    partner = me + 1 - 2 * core
+    pieces, height = stage_ref.shape[0], stage_ref.shape[1]
+    half = pieces * height
+    ring = [partner, lax.rem(me + 2, 2 * chips), lax.rem(me + 2 * chips - 2, 2 * chips)]
+    greet("tp", ring)
+
+    def rows(which, p):
+        return pl.ds(pl.multiple_of(which * half + p * height, height), height)
+
+    def remote(source, target, send, recv, device):
+        return pltpu.make_async_remote_copy(
+            src_ref=source,
+            dst_ref=target,
+            send_sem=send,
+            recv_sem=recv,
+            device_id={"tp": device},
+            device_id_type=LOGICAL,
+        )
+
+    def pair(p):
+        return remote(
+            part_ref.at[rows(1 - core, p), :], pair_ref.at[p], pair_send.at[p], pair_recv.at[p], partner
+        )
+
+    def rightward(p):
+        return remote(stage_ref.at[p], left_ref.at[p], line_send.at[p], left_recv.at[p], me + 2)
+
+    def leftward(p):
+        return remote(stage_ref.at[p], right_ref.at[p], line_send.at[p], right_recv.at[p], me - 2)
+
+    def outward(p, way):
+        mine = out_ref.at[rows(core, p), :]
+        return remote(mine, mine, out_send.at[way, p], out_recv.at[p], me + 4 * way - 2)
+
+    def share(p, which):
+        block = out_ref.at[rows(which, p), :]
+        return remote(block, block, share_send.at[p], share_recv.at[p], partner)
+
+    for p in range(pieces):
+        pair(p).start()
+
+    def run(z):
+        sent = []
+
+        def owner(p):
+            return chips // 2 - p % 2
+
+        def start(copy):
+            copy.start()
+            sent.append(copy)
+
+        def reduce(p):
+            pair(p).wait_recv()
+            value = part_ref[rows(core, p), :].astype(jnp.float32) + pair_ref[p].astype(jnp.float32)
+            if z > 0 and z <= owner(p):
+                rightward(p).wait_recv()
+                value = value + left_ref[p].astype(jnp.float32)
+            if z < chips - 1 and z >= owner(p):
+                leftward(p).wait_recv()
+                value = value + right_ref[p].astype(jnp.float32)
+            if z == owner(p):
+                total = value + base_ref[rows(core, p), :].astype(jnp.float32)
+                out_ref[rows(core, p), :] = total.astype(out_ref.dtype)
+                if z > 0:
+                    start(outward(p, 0))
+                if z < chips - 1:
+                    start(outward(p, 1))
+                start(share(p, core))
+            else:
+                stage_ref[p] = value.astype(stage_ref.dtype)
+                start(rightward(p) if z < owner(p) else leftward(p))
+
+        def spread(p):
+            if z == owner(p):
+                return
+            outward(p, 0).wait_recv()
+            if z < owner(p) and z > 0:
+                start(outward(p, 0))
+            if z > owner(p) and z < chips - 1:
+                start(outward(p, 1))
+            start(share(p, core))
+
+        lag = pieces if z in (0, chips - 1) else min(pieces, LAG)
+        for p in range(pieces + lag):
+            if p < pieces:
+                reduce(p)
+            if p >= lag:
+                spread(p - lag)
+        for copy in sent:
+            copy.wait_send()
+
+    for z in range(chips):
+        pl.when(chip == z)(functools.partial(run, z))
+    for p in range(pieces):
+        pair(p).wait_send()
+        share(p, 1 - core).wait_recv()
+
+
+def summed(part, base, call):
+    chips = lax.axis_size("tp") // 2
+    length, width = part.shape
+    pieces = length // (2 * HEIGHT)
+    vmem = pl.BlockSpec(memory_space=pltpu.VMEM)
+    block = pltpu.VMEM((pieces, HEIGHT, width), jnp.bfloat16)
+    semaphores = pltpu.SemaphoreType.DMA((pieces,))
+    return pl.pallas_call(
+        functools.partial(summed_kernel, chips),
+        out_shape=jax.ShapeDtypeStruct((length, width), jnp.bfloat16),
+        in_specs=[vmem] * 2,
+        out_specs=vmem,
+        scratch_shapes=[block] * 4
+        + [semaphores] * 5
+        + [pltpu.SemaphoreType.DMA((2, pieces))]
+        + [semaphores] * 3,
+        compiler_params=pltpu.CompilerParams(
+            collective_id=call, has_side_effects=True, vmem_limit_bytes=24 * 2**20
+        ),
+    )(part, base)
 
 
 def on_device(
@@ -222,8 +361,8 @@
         decay_bias,
         -8.0 * jax.nn.softplus(decay_param),
     )
-    mixed = channel_total(jnp.dot(gated, out_proj, preferred_element_type=jnp.float32))
-    middle = lax.optimization_barrier((residual.astype(jnp.float32) + mixed).astype(jnp.bfloat16))
+    mixed = jnp.dot(gated, out_proj, preferred_element_type=jnp.float32).astype(jnp.bfloat16)
+    middle = summed(mixed, residual, 1)
     hidden_in = rms_norm(middle, mlp_gain)
     width = gate_proj.shape[1]
     columns = lax.all_to_all(hidden_in, "seq", split_axis=1, concat_axis=0, tiled=True)
@@ -242,8 +381,8 @@
     gate = joined[:, :width]
     up = joined[:, width:]
     hidden = (jax.nn.gelu(gate, approximate=True) * up).astype(jnp.bfloat16)
-    output = channel_total(jnp.dot(hidden, down_proj, preferred_element_type=jnp.float32))
-    return (middle.astype(jnp.float32) + output).astype(jnp.bfloat16)
+    output = jnp.dot(hidden, down_proj, preferred_element_type=jnp.float32).astype(jnp.bfloat16)
+    return summed(output, middle, 2)
 
 
 def solution(mesh):

time: 294 us -> 294 us (level)
  Pallas kernels: 11.8 us -> 148 us
  waiting for transfers between devices: 198 us -> 68.9 us
  other arithmetic: 16.9 us -> 9.46 us
    pallas_call x0 -> x2, Pallas kernels: none -> 136 us  [summed(): pl.pallas_call(functools.partial(summed_kernel, chips), out_shape=jax.Sha...]
    psum x2 -> x0, waiting for transfers between devices: 131 us -> none  [channel_total(): lax.psum(partial_value.astype(jnp.bfloat16), 'tp').astype(jnp.float32)]
    convert_element_type x2 -> x0, other arithmetic: 7.33 us -> none  [the longest x1 4.32 us: on_device(): return (middle.astype(jnp.float32) + output).astype(jnp.bfloat16)]
  transfers between devices with their start and end apart: 3 -> 1, of which waited for: 3 -> 1; matrix products, arithmetic and copies ran while one was open for 0% -> 0% of each run, Pallas kernels for 0% -> 0%
where the time goes in v2:
time: 294 us
  Pallas kernels  148 us (50%)
  waiting for transfers between devices  68.9 us (23%)
  blocking collectives  28.6 us (10%)
  matrix products  22.8 us (8%)
  between operations  13.7 us (5%)
  other arithmetic  9.46 us (3%)
    pallas_call x2, Pallas kernels, summed(): pl.pallas_call(functools.partial(summed_kernel, chips), out_shape=jax.Sha...  136 us
    reduce_scatter x1, waiting for transfers between devices, summed_rows(): lax.psum_scatter(everything.astype(jnp.bfloat16), axis, scatter_dimension...  68.9 us
    all_to_all x1, blocking collectives, on_device(): lax.all_to_all(hidden_in, 'seq', split_axis=1, concat_axis=0, tiled=True)  28.6 us
    pallas_call x1, Pallas kernels, recurrence(): pl.pallas_call(functools.partial(recurrence_kernel, count, conv_weight.sh...  11.8 us
    dot_general x1, matrix products, on_device(): jnp.dot(hidden, down_proj, preferred_element_type=jnp.float32)  8.6 us
  transfers between devices with their start and end apart: 1, of which 1 were waited for; matrix products, arithmetic and copies ran while one was open for 0% of the time, Pallas kernels for 0%

profile of v2, /device:TPU:0, one launch (start us, length us, event | category | flops | bytes accessed | tf_op | source)
XLA Modules:
  0.0 293.8 jit_solution(2233204755587966448)
XLA Ops:
  6.5 2.2 fusion
  8.8 0.7 fusion.32
  9.5 4.3 %convolution_convert_fusion.4.inner_ref = bf16[256,512]{1,0:T(8,128)(2,1)S(1)} fusion(bf16[4096,512]{1,0:T(8,128)(2,1)} %param.18, bf16[256,4096]{1,0:T(8,128)(2,1)} %base_ref.1, f32[4096]{0:T(1024)} %param.17, f32[256]{0:T(256)S(1)} %add_rsqrt_fusion.1), kind=kOutput, calls=%fused_computation.26 | convolution fusion | flops 1078067200 | bytes 6571008 | tf_op jit(solution)/shard_map/dot_general | solution.py:352
  13.8 0.4 copy-done.12
  14.2 0.0 copy-start.8
  14.2 0.0 copy-start.9
  14.2 1.4 fusion.29.branch_ref
  15.7 11.8 %shard_map.154 = bf16[256,512]{1,0:T(8,128)(2,1)S(1)} custom-call(bf16[256,512]{1,0:T(8,128)(2,1)S(1)} %convolution_convert_fusion.4.inner_ref, f32[256,512]{1,0:T(8,128)S(1)} %fusion.29.branch_ref, f32[4,512]{1,0:T(4,128)S(1)} %copy-done.7, f32[1,512]{1,0:T(1,128)S(1)} %bitcast.21, bf16[2,256,256]{2,1,0:T(8,128)(2,1)S(1)} %copy-done.5, ...), custom_call_target="tpu_custom_call" | custom-call | tf_op jit(solution)/shard_map/pallas_call | solution.py:144
  27.6 1.3 convolution_convert_fusion.1.part_ref
  28.9 68.6 %shard_map.155.base_ref = bf16[256,4096]{1,0:T(8,128)(2,1)S(1)} custom-call(bf16[256,4096]{1,0:T(8,128)(2,1)S(1)} %convolution_convert_fusion.1.part_ref, bf16[256,4096]{1,0:T(8,128)(2,1)S(1)} %copy-done.4), custom_call_target="tpu_custom_call" | custom-call | tf_op jit(solution)/shard_map/pallas_call | solution.py:314
  97.5 0.5 fusion.3
  98.0 0.6 fusion.5
  98.6 0.2 copy-done.2
  98.8 0.2 copy.20
  99.0 28.6 %all_to_all.19 = bf16[256,4,1024]{2,0,1:T(8,128)(2,1)S(1)} all-to-all(bf16[256,4,1024]{2,0,1:T(8,128)(2,1)S(1)} %bitcast.25), channel_id=1, replica_groups=mesh['tp'=8,'seq'=4] {'seq'}, dimensions={1} | all-to-all | bytes 4194304 | tf_op jit(solution)/shard_map/all_to_all | solution.py:368
  127.6 3.6 %convolution_convert_fusion.2 = bf16[1024,1536]{1,0:T(8,128)(2,1)S(1)} fusion(bf16[1024,1024]{1,0:T(8,128)(2,1)S(1)} %bitcast.26, bf16[1024,1536]{1,0:T(8,128)(2,1)S(1)} %copy-done), kind=kOutput, calls=%fused_computation.13 | convolution fusion | flops 3222798336 | bytes 8388608 | tf_op jit(solution)/shard_map/dot_general | solution.py:375
  131.3 3.6 %convolution_convert_fusion.3 = bf16[1024,1536]{1,0:T(8,128)(2,1)S(1)} fusion(bf16[1024,1024]{1,0:T(8,128)(2,1)S(1)} %bitcast.27, bf16[1024,1536]{1,0:T(8,128)(2,1)S(1)} %copy-done.14), kind=kOutput, calls=%fused_computation.14 | convolution fusion | flops 3222798336 | bytes 8388608 | tf_op jit(solution)/shard_map/dot_general | solution.py:374
  134.9 3.6 %pad_maximum_fusion = bf16[1024,3072]{1,0:T(8,128)(2,1)} fusion(bf16[1024,1536]{1,0:T(8,128)(2,1)S(1)} %convolution_convert_fusion.2, bf16[1024,1536]{1,0:T(8,128)(2,1)S(1)} %convolution_convert_fusion.3), kind=kLoop, calls=%fused_computation | loop fusion | flops 12582912 | bytes 12582912 | tf_op jit(solution)/shard_map/concatenate | solution.py:372
  138.5 0.0 reduce-scatter.2.cloned.1.call-update
  138.6 68.9 %reduce-scatter.2.cloned.1.call-done = bf16[256,3072]{1,0:T(8,128)(2,1)} async-done(((bf16[1024,3072]{1,0:T(8,128)(2,1)}), bf16[256,3072]{1,0:T(8,128)(2,1)}) %reduce-scatter.2.cloned.1.call-update) | async-done | bytes 1572880 | tf_op jit(solution)/shard_map/reduce_scatter | solution.py:178
  207.5 1.8 convert_element_type.34
  209.3 8.6 %convolution_convert_fusion.part_ref = bf16[256,4096]{1,0:T(8,128)(2,1)S(1)} fusion(bf16[1536,4096]{1,0:T(8,128)(2,1)} %param.31, f32[256,3072]{1,0:T(8,128)S(1)} %convert_element_type.34), kind=kOutput, calls=%fused_computation.5 | convolution fusion | flops 3226206208 | bytes 17825792 | tf_op jit(solution)/shard_map/dot_general | solution.py:384
  217.9 67.7 %shard_map.156 = bf16[256,4096]{1,0:T(8,128)(2,1)S(1)} custom-call(bf16[256,4096]{1,0:T(8,128)(2,1)S(1)} %convolution_convert_fusion.part_ref, bf16[256,4096]{1,0:T(8,128)(2,1)S(1)} %copy-done.3), custom_call_target="tpu_custom_call" | custom-call | tf_op jit(solution)/shard_map/pallas_call | solution.py:314
  285.6 1.3 copy.22
  (31 shorter events, 0.1 us)
Async XLA Ops:
  6.5 121.1 %copy-start = (bf16[1024,1536]{1,0:T(8,128)(2,1)S(1)}, bf16[1024,1536]{1,0:T(8,128)(2,1)}, u32[]{:S(2)}) copy-start(bf16[1024,1536]{1,0:T(8,128)(2,1)} %param.30) | copy-start | bytes 9437188
  6.5 200.9 %reduce-scatter.2.cloned.1.call-start = ((), (), s32[]{:S(2)}) async-start(), calls=%async_computation.2 | async-start | bytes 7864320 | tf_op jit(solution)/shard_map/reduce_scatter | solution.py:178
  9.5 4.3 %copy-start.4 = (bf16[256,4096]{1,0:T(8,128)(2,1)S(1)}, bf16[256,4096]{1,0:T(8,128)(2,1)}, u32[]{:S(2)}) copy-start(bf16[256,4096]{1,0:T(8,128)(2,1)} %base_ref.1) | copy-start | bytes 6291460
  9.5 4.7 %copy-start.12 = (bf16[4096,512]{1,0:T(8,128)(2,1)S(1)}, bf16[4096,512]{1,0:T(8,128)(2,1)}, u32[]{:S(2)}) copy-start(bf16[4096,512]{1,0:T(8,128)(2,1)} %param.19) | copy-start | bytes 12582916
  9.5 4.7 %copy-start.15 = (f32[4096]{0:T(1024)S(1)}, f32[4096]{0:T(1024)}, u32[]{:S(2)}) copy-start(f32[4096]{0:T(1024)} %param.17) | copy-start | bytes 49156
  14.2 1.5 copy-start.5
  14.2 1.5 copy-start.6
  14.2 1.5 copy-start.7
  14.2 1.5 copy-start.8
  14.2 1.5 copy-start.9
  14.2 1.5 copy-start.10
  14.2 13.3 %copy-start.13 = (bf16[512,4096]{1,0:T(8,128)(2,1)S(1)}, bf16[512,4096]{1,0:T(8,128)(2,1)}, u32[]{:S(2)}) copy-start(bf16[512,4096]{1,0:T(8,128)(2,1)} %param.27) | copy-start | bytes 12582916
  28.8 69.1 %copy-start.11 = (f32[4096]{0:T(1024)S(1)}, f32[4096]{0:T(1024)}, u32[]{:S(2)}) copy-start(f32[4096]{0:T(1024)} %param.28) | copy-start | bytes 49156
  97.4 1.3 copy-start.2
  127.6 3.6 %copy-start.14 = (bf16[1024,1536]{1,0:T(8,128)(2,1)S(1)}, bf16[1024,1536]{1,0:T(8,128)(2,1)}, u32[]{:S(2)}) copy-start(bf16[1024,1536]{1,0:T(8,128)(2,1)} %param.29) | copy-start | bytes 9437188
  209.3 8.6 %copy-start.3 = (bf16[256,4096]{1,0:T(8,128)(2,1)S(1)}, bf16[256,4096]{1,0:T(8,128)(2,1)}, u32[]{:S(2)}) copy-start(bf16[256,4096]{1,0:T(8,128)(2,1)} %copy-done.2) | copy-start | bytes 6291460
  217.9 69.0 %copy-start.1 = (bf16[1024,1536]{1,0:T(8,128)(2,1)S(1)}, bf16[1024,1536]{1,0:T(8,128)(2,1)}, u32[]{:S(2)}) copy-start(bf16[1024,1536]{1,0:T(8,128)(2,1)} %param.30) | copy-start | bytes 9437188
Sparse Core Ops, SparseCore 0:
  138.7 68.7 reduce-scatter.1
